TPU v7x, 32 devices: a whole 2x2x4 slice. The times are simulated.
32 devices in a mesh: seq: 8 (over z, y), tp: 4 (over x, core).
Axes of the slice: x: 2, y: 2, z: 4, core: 2. Of those that a mesh axis runs over, the one named last changes fastest.
Arguments:
- ssm_inputs: bfloat16 [8192, 8192], P('seq', 'tp'), may hold values from -6 to 6
- step_sizes: float32 [8192, 128], P('seq', 'tp'), as said below
- decay_rates: float32 [128], P('tp'), as said below
- state_inputs: bfloat16 [8192, 128], P('seq'), may hold values from -6 to 6
- state_readout: bfloat16 [8192, 128], P('seq'), may hold values from -0.5 to 0.5
- skip_gain: float32 [128], P('tp'), may hold values from 0.5 to 1.5
- mixed_inputs: bfloat16 [1536, 8192], P('seq', 'tp'), may hold values from -6 to 6
- out_weight: bfloat16 [8192, 8192], P('tp', 'seq'), may hold values from -0.0625 to 0.0625
Outputs:
- ssm_output: bfloat16 [8192, 8192], P('seq', 'tp')
- projected: bfloat16 [1536, 8192], P('seq', 'tp')
Inputs may be any that keep to these rules, and one draw needn't show every extreme that they name: `step_sizes`: all entries are positive. `decay_rates`: all entries are positive.
All inputs are finite; a program needn't handle non-finite values.
Results may differ from a plain program's by a relative error of at most 0.017.
Values may be sent and summed in bfloat16 or wider, within the bound.
A program may use at most 192 MiB of HBM per device.

v0:
```python
import jax
import jax.numpy as jnp
from jax import lax
from jax.sharding import PartitionSpec as P

HEAD_DIM = 64
STATE = 128
SPAN = 256


def carried_in(array, axis, join, neutral):
    place = lax.axis_index(axis)
    gathered = jax.tree.map(
        lambda a, kind: lax.all_gather(a.astype(kind), axis), array, (jnp.bfloat16, jnp.bfloat16)
    )
    state = jax.tree.map(lambda a, e: jnp.zeros_like(a) + jnp.asarray(e, a.dtype), array, neutral)

    def one(lap, state):
        return join(
            state,
            jax.tree.map(
                lambda a, own: lax.dynamic_index_in_dim(a, lap, 0, False).astype(own.dtype),
                gathered,
                array,
            ),
        )

    return lax.fori_loop(0, place, one, state)


def combine(earlier, latter):
    return (earlier[0] * latter[0], latter[0][:, None, None] * earlier[1] + latter[1])


def per_device(
    ssm_inputs,
    step_sizes,
    decay_rates,
    state_inputs,
    state_readout,
    skip_gain,
    mixed_inputs,
    out_weight,
):
    row_count = ssm_inputs.shape[0]
    head_count = step_sizes.shape[1]
    block_count = row_count // SPAN
    x_blocks = ssm_inputs.reshape(block_count, SPAN, head_count, HEAD_DIM)
    dt_blocks = step_sizes.reshape(block_count, SPAN, head_count)
    b_blocks = state_inputs.reshape(block_count, SPAN, STATE)
    c_blocks = state_readout.reshape(block_count, SPAN, STATE)
    log_decay = jnp.cumsum(-decay_rates[None, None, :] * dt_blocks, axis=1)
    block_decay = log_decay[:, -1, :]
    tail_weight = jnp.exp(block_decay[:, None, :] - log_decay) * dt_blocks
    weighted = (tail_weight[..., None] * x_blocks).astype(jnp.bfloat16)
    block_states = jnp.einsum(
        "cshp,csn->chpn", weighted, b_blocks, preferred_element_type=jnp.float32
    )
    carried = jnp.zeros((head_count, HEAD_DIM, STATE), jnp.float32)
    entering = []
    for block_id in range(block_count):
        entering.append(carried)
        carried = jnp.exp(block_decay[block_id])[:, None, None] * carried + block_states[block_id]
    total_decay = jnp.exp(jnp.sum(block_decay, axis=0))
    identity = (jnp.ones_like(total_decay), jnp.zeros_like(carried))
    decay_before, state_before = carried_in((total_decay, carried), "seq", combine, identity)
    prior_decay = jnp.exp(jnp.cumsum(block_decay, axis=0) - block_decay)
    entering_all = jnp.stack(entering) + prior_decay[:, :, None, None] * state_before[None]
    entering_rounded = entering_all.astype(jnp.bfloat16)
    readout = jnp.einsum(
        "ctn,chpn->cthp", c_blocks, entering_rounded, preferred_element_type=jnp.float32
    )
    y_off = jnp.exp(log_decay)[..., None] * readout
    gram = jnp.einsum("ctn,csn->cts", c_blocks, b_blocks, preferred_element_type=jnp.float32)
    per_head = jnp.transpose(log_decay, (0, 2, 1))
    differ = per_head[:, :, :, None] - per_head[:, :, None, :]
    lower = jnp.tril(jnp.ones((SPAN, SPAN), dtype=bool))
    decay = jnp.exp(jnp.where(lower[None, None], differ, -jnp.inf))
    dt_heads = jnp.transpose(dt_blocks, (0, 2, 1))
    scores = (gram[:, None] * decay * dt_heads[:, :, None, :]).astype(jnp.bfloat16)
    y_diag = jnp.einsum("chts,cshp->cthp", scores, x_blocks, preferred_element_type=jnp.float32)
    combined = y_diag + y_off + skip_gain[None, None, :, None] * x_blocks
    ssm_output = combined.astype(jnp.bfloat16).reshape(row_count, head_count * HEAD_DIM)
    spread_rows = jnp.dot(
        lax.all_gather(mixed_inputs, "seq", axis=0, tiled=True),
        out_weight,
        preferred_element_type=jnp.float32,
    )
    regrouped = lax.all_to_all(
        spread_rows.astype(jnp.bfloat16), "seq", split_axis=0, concat_axis=1, tiled=True
    )
    group_terms = regrouped.astype(jnp.float32)
    projected = lax.psum_scatter(
        group_terms.astype(jnp.bfloat16), "tp", scatter_dimension=1, tiled=True
    )
    return (ssm_output, projected)


def solution(mesh):
    in_specs = (
        P("seq", "tp"),
        P("seq", "tp"),
        P("tp"),
        P("seq", None),
        P("seq", None),
        P("tp"),
        P("seq", "tp"),
        P("tp", "seq"),
    )
    out_specs = (P("seq", "tp"), P("seq", "tp"))
    return jax.shard_map(
        per_device, mesh=mesh, in_specs=in_specs, out_specs=out_specs, check_vma=False
    )
```

profile of v0, /device:TPU:28, one launch (start us, length us, event | category | flops | bytes accessed | tf_op | source)
XLA Modules:
  0.0 322.4 jit_solution(16475436109490359027)
XLA Ops:
  7.2 0.0 copy-start
  7.2 0.0 all-gather.6.cloned.1.call-start
  7.2 0.7 all-gather.6.cloned.1.call-update
  7.9 0.0 all-gather.4.cloned.1.call-start
  8.0 1.0 reshape.138
  8.9 0.7 neg.4
  9.6 0.1 multiply_bitcast_fusion
  9.7 0.1 reshape.153
  9.8 2.3 reduce-window.6
  12.2 0.1 slice.52
  12.3 0.1 copy.63
  12.4 12.9 %reshape.155 = bf16[4,256,32,64]{3,2,1,0:T(8,128)(2,1)} reshape(bf16[1024,2048]{1,0:T(8,128)(2,1)} %param.10) | data formatting | bytes 8388608 | tf_op jit(solution)/shard_map/reshape | solution.py:48
  25.3 0.0 copy-start.2
  25.3 0.0 copy-start.1
  25.3 10.4 %copy.68 = bf16[4,256,32,64]{1,3,2,0:T(8,128)(2,1)} copy(bf16[4,256,32,64]{3,2,1,0:T(8,128)(2,1)} %reshape.155) | data formatting | bytes 8388608 | tf_op jit(solution)/shard_map/reshape | solution.py:48
  35.8 0.1 fusion.29
  35.9 0.2 fusion.20
  36.1 0.2 slice_reduce_fusion
  36.3 0.0 copy-done.2
  36.3 0.1 bitcast_multiply_fusion.1
  36.5 0.0 copy-done.1
  36.5 3.5 %fusion.11 = f32[4,32,64,128]{3,2,1,0:T(8,128)S(1)} fusion(bf16[4,256,128,1]{2,1,3,0:T(8,128)(2,1)S(1)} %bitcast.77, bf16[4,256,32,64]{1,3,2,0:T(8,128)(2,1)} %copy.68, f32[4,256,32]{1,2,0:T(8,128)S(1)} %get-tuple-element.75), kind=kOutput, calls=%fused_computation.17 | convolution fusion | flops 543162368 | bytes 8781824 | tf_op jit(solution)/shard_map/cshp,csn->chpn/dot_general | solution.py:56
  40.0 1.5 fusion.19
  41.5 0.0 all-gather.4.cloned.1.call-update
  41.5 0.0 reduce-scatter.2.cloned.1.call-start
  41.5 65.5 %all-gather.6.cloned.1.call-done = bf16[1536,2048]{1,0:T(8,128)(2,1)} async-done(((bf16[192,2048]{1,0:T(8,128)(2,1)}), bf16[1536,2048]{1,0:T(8,128)(2,1)}) %all-gather.6.cloned.1.call-update) | async-done | bytes 6291472 | tf_op jit(solution)/shard_map/all_gather | solution.py:85
  107.0 10.0 %convolution_convert_fusion = bf16[1536,1024]{1,0:T(8,128)(2,1)S(1)} fusion(bf16[1536,2048]{1,0:T(8,128)(2,1)} %all-gather.6.cloned.1.call-done, bf16[2048,1024]{1,0:T(8,128)(2,1)} %param.17), kind=kOutput, calls=%fused_computation.21 | convolution fusion | flops 6444023808 | bytes 13631488 | tf_op jit(solution)/shard_map/dot_general | solution.py:84
  117.0 121.2 %all_to_all.19 = bf16[8,192,1024]{2,1,0:T(8,128)(2,1)S(1)} all-to-all(bf16[8,192,1024]{2,1,0:T(8,128)(2,1)S(1)} %bitcast.76), channel_id=1, replica_groups=mesh['seq'=8,'tp'=4] {'seq'}, dimensions={0} | all-to-all | bytes 6291456 | tf_op jit(solution)/shard_map/all_to_all | solution.py:89
  238.2 0.0 copy-start.4
  238.2 2.1 copy.84
  240.3 0.0 reduce-scatter.2.cloned.1.call-update
  240.4 0.0 copy-done.4
  240.4 0.6 dynamic-slice
  241.6 0.2 dynamic-update-slice
  241.8 16.9 %all-reduce = bf16[256]{0:T(256)(128)(2,1)S(1)} all-reduce(bf16[256]{0:T(256)(128)(2,1)S(1)} %dynamic-update-slice), channel_id=2, replica_groups=mesh['seq'=8,'tp'=4] {'seq'}, use_global_device_ids=true, to_apply=%add | all-reduce | flops 256 | bytes 1024
  258.7 0.1 reshape.145
  258.9 0.0 copy-done
  258.9 0.3 fusion.30
  259.2 12.6 %fusion = f32[4,32,256,64]{2,3,1,0:T(8,128)} fusion(bf16[4,256,32,64]{1,3,2,0:T(8,128)(2,1)} %copy.68, f32[4,32,256]{2,1,0:T(8,128)S(1)} %copy.66, f32[4,32,256]{2,1,0:T(8,128)S(1)} %get-tuple-element.78, f32[4,256,256]{2,1,0:T(8,128)S(1)} %fusion.30, pred[256,256]{1,0:T(8,128)(4,1)S(1)} %iota_compare_fusion), kind=kOutput, calls=%fused_computation.3 | convolution fusion | flops 1115684864 | bytes 13959168 | tf_op jit(solution)/shard_map/chts,cshp->cthp/dot_general | solution.py:81
  271.8 0.0 all-gather.4.cloned.1.call-done
  271.8 0.1 broadcast.34
  271.9 0.0 copy-start.3
  271.9 9.7 %while.12 = (s32[]{:T(128)}, f32[32,64,128]{2,1,0:T(8,128)S(1)}, s32[]{:T(128)}, bf16[8,32]{1,0:T(8,128)(2,1)S(1)}, bf16[8,32,64,128]{3,2,1,0:T(8,128)(2,1)}, /*index=5*/s32[]{:T(128)}, s32[]{:T(128)}, s32[]{:T(128)}) while((s32[]{:T(128)}, f32[32,64,128]{2,1,0:T(8,128)S(1)}, s32[]{:T(128)}, bf16[8,32]{1,0:T(8,128)(2,1)S(1)}, ...), condition=%wide.region_5.6_spmd, body=%wide.region_4.5_spmd.sunk | while | flops 786469 | bytes 2621887 | solution.py:28
  272.0 1.3 convert_add_fusion.2
  273.3 1.3 convert_add_fusion.2
  274.7 1.3 convert_add_fusion.2
  276.0 1.3 convert_add_fusion.2
  277.4 1.3 convert_add_fusion.2
  278.7 1.3 convert_add_fusion.2
  280.1 1.3 convert_add_fusion.2
  281.6 0.0 copy-done.3
  281.6 9.0 %fusion.9 = bf16[4,256,32,64]{1,3,2,0:T(8,128)(2,1)} fusion(bf16[4,256,32,64]{1,3,2,0:T(8,128)(2,1)} %copy.68, f32[4,32,256,64]{2,3,1,0:T(8,128)} %fusion, f32[32]{0:T(128)S(1)} %copy-done.3, f32[4,256,32]{1,2,0:T(8,128)S(1)} %get-tuple-element.76, bf16[4,256,128,1]{2,1,3,0:T(8,128)(2,1)S(1)} %bitcast.73, f32[1,32,64,128]{3,2,1,0:T(8,128)S(1)} %get-tuple-element.72, ...), kind=kOutput, calls=%fused_computation.14 | convolution fusion | flops 555745280 | bytes 21365392 | tf_op jit(solution)/shard_map/ctn,chpn->cthp/dot_general | solution.py:70
  290.7 12.9 %copy.78 = bf16[4,256,32,64]{3,2,1,0:T(8,128)(2,1)} copy(bf16[4,256,32,64]{1,3,2,0:T(8,128)(2,1)} %fusion.9) | data formatting | bytes 8388608
  303.6 12.3 %reshape.154 = bf16[1024,2048]{1,0:T(8,128)(2,1)} reshape(bf16[4,256,32,64]{3,2,1,0:T(8,128)(2,1)} %copy.78) | data formatting | bytes 8388608
  315.9 0.0 reduce-scatter.2.cloned.1.call-done
  (18 shorter events, 0.2 us)
Async XLA Ops:
  7.2 251.7 %copy-start = (bf16[1024,128]{1,0:T(8,128)(2,1)S(1)}, bf16[1024,128]{1,0:T(8,128)(2,1)}, u32[]{:S(2)}) copy-start(bf16[1024,128]{1,0:T(8,128)(2,1)} %param.14) | copy-start | bytes 786436
  7.2 99.8 %all-gather.6.cloned.1.call-start = ((), (), s32[]{:S(2)}) async-start(), calls=%async_computation.3 | async-start | bytes 7077888 | tf_op jit(solution)/shard_map/all_gather | solution.py:85
  7.9 263.9 %all-gather.4.cloned.1.call-start = ((), (), s32[]{:S(2)}) async-start(), calls=%async_computation.2 | async-start | bytes 4718592 | tf_op jit(solution)/shard_map/all_gather | solution.py:14
  25.3 11.0 %copy-start.2 = (f32[1024,32]{0,1:T(8,128)S(1)}, f32[1024,32]{0,1:T(8,128)}, u32[]{:S(2)}) copy-start(f32[1024,32]{0,1:T(8,128)} %param.11) | copy-start | bytes 393220
  25.3 11.1 %copy-start.1 = (bf16[1024,128]{1,0:T(8,128)(2,1)S(1)}, bf16[1024,128]{1,0:T(8,128)(2,1)}, u32[]{:S(2)}) copy-start(bf16[1024,128]{1,0:T(8,128)(2,1)} %param.13) | copy-start | bytes 786436
  41.5 274.4 %reduce-scatter.2.cloned.1.call-start = ((), (), s32[]{:S(2)}) async-start(), calls=%async_computation.4 | async-start | bytes 3932160 | tf_op jit(solution)/shard_map/reduce_scatter | solution.py:93
  238.2 2.2 copy-start.4
  271.9 9.7 %copy-start.3 = (f32[32]{0:T(128)S(1)}, f32[32]{0:T(128)}, u32[]{:S(2)}) copy-start(f32[32]{0:T(128)} %param.15) | copy-start | bytes 388
Sparse Core Ops, SparseCore 0:
  10.2 96.8 all-gather.5
  109.1 121.5 all-gather.3
  240.5 38.6 reduce-scatter.1
where the time goes:
time: 324 us; the launch traced here: 322 us
  blocking collectives  138 us (43%)
  waiting for transfers between devices  66.2 us (20%)
  local copies, waits for them, and re-layouts  53.1 us (16%)
  matrix products  35.4 us (11%)
  other arithmetic  14.5 us (4%)
  between operations  14.5 us (4%)
    all_to_all x1, blocking collectives, per_device(): lax.all_to_all(spread_rows.astype(jnp.bfloat16), 'seq', split_axis=0, con...  121 us
    all_gather x1, waiting for transfers between devices, per_device(): lax.all_gather(mixed_inputs, 'seq', axis=0, tiled=True)  65.5 us
    unnamed x15, local copies, waits for them, and re-layouts  26.1 us
    reshape x2, local copies, waits for them, and re-layouts, per_device(): x_blocks = ssm_inputs.reshape(block_count, SPAN, head_count, HEAD_DIM)  23.4 us
    unnamed x1, blocking collectives  16.9 us
    dot_general x1, matrix products, per_device(): jnp.einsum('chts,cshp->cthp', scores, x_blocks, preferred_element_type=jn...  12.6 us
    dot_general x1, matrix products, per_device(): jnp.dot(lax.all_gather(mixed_inputs, 'seq', axis=0, tiled=True), out_weig...  10 us
    add x7, other arithmetic, combine(): latter[0][:, None, None] * earlier[1] + latter[1]  9.14 us
  transfers between devices with their start and end apart: 3, of which 1 were waited for; matrix products, arithmetic and copies ran while one was open for 32% of the time, Pallas kernels for 0%

commit v1 on v0

--- a/solution.py
+++ b/solution.py
@@ -86,8 +86,14 @@
         out_weight,
         preferred_element_type=jnp.float32,
     )
-    regrouped = lax.all_to_all(
-        spread_rows.astype(jnp.bfloat16), "seq", split_axis=0, concat_axis=1, tiled=True
+    regrouped = jnp.concatenate(
+        lax.all_to_all(
+            jnp.stack(jnp.split(spread_rows.astype(jnp.bfloat16), lax.axis_size("seq"), axis=0)),
+            "seq",
+            0,
+            0,
+        ),
+        axis=1,
     )
     group_terms = regrouped.astype(jnp.float32)
     projected = lax.psum_scatter(

time: 324 us -> 324 us (level)
    unnamed x15 -> x22, local copies, waits for them, and re-layouts: 26.1 us -> 26.3 us
where the time goes in v1:
time: 324 us; the launch traced here: 322 us
  blocking collectives  138 us (43%)
  waiting for transfers between devices  66.2 us (20%)
  local copies, waits for them, and re-layouts  53.3 us (16%)
  matrix products  35.4 us (11%)
  between operations  14.6 us (5%)
  other arithmetic  14.5 us (4%)
    all_to_all x1, blocking collectives, per_device(): lax.all_to_all(jnp.stack(jnp.split(spread_rows.astype(jnp.bfloat16), lax....  121 us
    all_gather x1, waiting for transfers between devices, per_device(): lax.all_gather(mixed_inputs, 'seq', axis=0, tiled=True)  65.5 us
    unnamed x22, local copies, waits for them, and re-layouts  26.3 us
    reshape x2, local copies, waits for them, and re-layouts, per_device(): x_blocks = ssm_inputs.reshape(block_count, SPAN, head_count, HEAD_DIM)  23.4 us
    unnamed x1, blocking collectives  16.9 us
    dot_general x1, matrix products, per_device(): jnp.einsum('chts,cshp->cthp', scores, x_blocks, preferred_element_type=jn...  12.6 us
    dot_general x1, matrix products, per_device(): jnp.dot(lax.all_gather(mixed_inputs, 'seq', axis=0, tiled=True), out_weig...  10 us
    add x7, other arithmetic, combine(): latter[0][:, None, None] * earlier[1] + latter[1]  9.14 us
  transfers between devices with their start and end apart: 3, of which 1 were waited for; matrix products, arithmetic and copies ran while one was open for 32% of the time, Pallas kernels for 0%

profile of v1, /device:TPU:28, one launch (start us, length us, event | category | flops | bytes accessed | tf_op | source)
XLA Modules:
  0.0 322.4 jit_solution(15978366350210241653)
XLA Ops:
  7.2 0.0 copy-start
  7.2 0.0 all-gather.6.cloned.1.call-start
  7.2 0.7 all-gather.6.cloned.1.call-update
  7.9 0.0 all-gather.4.cloned.1.call-start
  8.0 1.0 reshape.141
  8.9 0.7 neg.4
  9.6 0.1 multiply_bitcast_fusion
  9.7 0.1 reshape.158
  9.8 2.3 reduce-window.6
  12.2 0.1 slice.52
  12.3 0.1 copy.62
  12.4 12.9 %reshape.160 = bf16[4,256,32,64]{3,2,1,0:T(8,128)(2,1)} reshape(bf16[1024,2048]{1,0:T(8,128)(2,1)} %param.10) | data formatting | bytes 8388608 | tf_op jit(solution)/shard_map/reshape | solution.py:48
  25.3 0.0 copy-start.2
  25.3 0.0 copy-start.1
  25.3 10.4 %copy.67 = bf16[4,256,32,64]{1,3,2,0:T(8,128)(2,1)} copy(bf16[4,256,32,64]{3,2,1,0:T(8,128)(2,1)} %reshape.160) | data formatting | bytes 8388608 | tf_op jit(solution)/shard_map/reshape | solution.py:48
  35.8 0.1 fusion.37
  35.9 0.2 fusion.28
  36.1 0.2 slice_reduce_fusion
  36.3 0.0 copy-done.2
  36.3 0.1 bitcast_multiply_fusion.1
  36.5 0.0 copy-done.1
  36.5 3.5 %fusion.11 = f32[4,32,64,128]{3,2,1,0:T(8,128)S(1)} fusion(bf16[4,256,128,1]{2,1,3,0:T(8,128)(2,1)S(1)} %bitcast.107, bf16[4,256,32,64]{1,3,2,0:T(8,128)(2,1)} %copy.67, f32[4,256,32]{1,2,0:T(8,128)S(1)} %get-tuple-element.75), kind=kOutput, calls=%fused_computation.17 | convolution fusion | flops 543162368 | bytes 8781824 | tf_op jit(solution)/shard_map/cshp,csn->chpn/dot_general | solution.py:56
  40.0 1.5 fusion.19
  41.5 0.0 all-gather.4.cloned.1.call-update
  41.5 0.0 reduce-scatter.2.cloned.1.call-start
  41.5 65.5 %all-gather.6.cloned.1.call-done = bf16[1536,2048]{1,0:T(8,128)(2,1)} async-done(((bf16[192,2048]{1,0:T(8,128)(2,1)}), bf16[1536,2048]{1,0:T(8,128)(2,1)}) %all-gather.6.cloned.1.call-update) | async-done | bytes 6291472 | tf_op jit(solution)/shard_map/all_gather | solution.py:85
  107.0 10.0 %convolution_convert_fusion = bf16[1536,1024]{1,0:T(8,128)(2,1)S(1)} fusion(bf16[1536,2048]{1,0:T(8,128)(2,1)} %all-gather.6.cloned.1.call-done, bf16[2048,1024]{1,0:T(8,128)(2,1)} %param.17), kind=kOutput, calls=%fused_computation.21 | convolution fusion | flops 6444023808 | bytes 13631488 | tf_op jit(solution)/shard_map/dot_general | solution.py:84
  117.3 120.9 %all_to_all.5 = bf16[8,192,1024]{2,1,0:T(8,128)(2,1)S(1)} all-to-all(bf16[8,192,1024]{2,1,0:T(8,128)(2,1)S(1)} %fusion.20), channel_id=1, replica_groups=mesh['seq'=8,'tp'=4] {'seq'}, dimensions={0} | all-to-all | bytes 6291456 | tf_op jit(solution)/shard_map/all_to_all | solution.py:90
  238.2 0.0 copy-start.4
  238.2 2.1 copy.83
  240.3 0.0 reduce-scatter.2.cloned.1.call-update
  240.4 0.0 copy-done.4
  240.4 0.6 dynamic-slice
  241.5 0.2 dynamic-update-slice
  241.8 16.9 %all-reduce = bf16[256]{0:T(256)(128)(2,1)S(1)} all-reduce(bf16[256]{0:T(256)(128)(2,1)S(1)} %dynamic-update-slice), channel_id=2, replica_groups=mesh['seq'=8,'tp'=4] {'seq'}, use_global_device_ids=true, to_apply=%add | all-reduce | flops 256 | bytes 1024
  258.7 0.1 reshape.150
  258.9 0.0 copy-done
  258.9 0.3 fusion.38
  259.2 12.6 %fusion = f32[4,32,256,64]{2,3,1,0:T(8,128)} fusion(bf16[4,256,32,64]{1,3,2,0:T(8,128)(2,1)} %copy.67, f32[4,32,256]{2,1,0:T(8,128)S(1)} %copy.65, f32[4,32,256]{2,1,0:T(8,128)S(1)} %get-tuple-element.78, f32[4,256,256]{2,1,0:T(8,128)S(1)} %fusion.38, pred[256,256]{1,0:T(8,128)(4,1)S(1)} %iota_compare_fusion), kind=kOutput, calls=%fused_computation.3 | convolution fusion | flops 1115684864 | bytes 13959168 | tf_op jit(solution)/shard_map/chts,cshp->cthp/dot_general | solution.py:81
  271.8 0.0 all-gather.4.cloned.1.call-done
  271.8 0.1 broadcast.34
  271.9 0.0 copy-start.3
  271.9 9.7 %while.12 = (s32[]{:T(128)}, f32[32,64,128]{2,1,0:T(8,128)S(1)}, s32[]{:T(128)}, bf16[8,32]{1,0:T(8,128)(2,1)S(1)}, bf16[8,32,64,128]{3,2,1,0:T(8,128)(2,1)}, /*index=5*/s32[]{:T(128)}, s32[]{:T(128)}, s32[]{:T(128)}) while((s32[]{:T(128)}, f32[32,64,128]{2,1,0:T(8,128)S(1)}, s32[]{:T(128)}, bf16[8,32]{1,0:T(8,128)(2,1)S(1)}, ...), condition=%wide.region_5.6_spmd, body=%wide.region_4.5_spmd.sunk | while | flops 786469 | bytes 2621887 | solution.py:28
  272.0 1.3 convert_add_fusion.2
  273.3 1.3 convert_add_fusion.2
  274.7 1.3 convert_add_fusion.2
  276.0 1.3 convert_add_fusion.2
  277.4 1.3 convert_add_fusion.2
  278.7 1.3 convert_add_fusion.2
  280.1 1.3 convert_add_fusion.2
  281.6 0.0 copy-done.3
  281.6 9.0 %fusion.9 = bf16[4,256,32,64]{1,3,2,0:T(8,128)(2,1)} fusion(bf16[4,256,32,64]{1,3,2,0:T(8,128)(2,1)} %copy.67, f32[4,32,256,64]{2,3,1,0:T(8,128)} %fusion, f32[32]{0:T(128)S(1)} %copy-done.3, f32[4,256,32]{1,2,0:T(8,128)S(1)} %get-tuple-element.76, bf16[4,256,128,1]{2,1,3,0:T(8,128)(2,1)S(1)} %bitcast.104, f32[1,32,64,128]{3,2,1,0:T(8,128)S(1)} %get-tuple-element.72, ...), kind=kOutput, calls=%fused_computation.14 | convolution fusion | flops 555745280 | bytes 21365392 | tf_op jit(solution)/shard_map/ctn,chpn->cthp/dot_general | solution.py:70
  290.6 12.9 %copy.77 = bf16[4,256,32,64]{3,2,1,0:T(8,128)(2,1)} copy(bf16[4,256,32,64]{1,3,2,0:T(8,128)(2,1)} %fusion.9) | data formatting | bytes 8388608
  303.6 12.3 %reshape.159 = bf16[1024,2048]{1,0:T(8,128)(2,1)} reshape(bf16[4,256,32,64]{3,2,1,0:T(8,128)(2,1)} %copy.77) | data formatting | bytes 8388608
  315.9 0.0 reduce-scatter.2.cloned.1.call-done
  (26 shorter events, 0.4 us)
Async XLA Ops:
  7.2 251.7 %copy-start = (bf16[1024,128]{1,0:T(8,128)(2,1)S(1)}, bf16[1024,128]{1,0:T(8,128)(2,1)}, u32[]{:S(2)}) copy-start(bf16[1024,128]{1,0:T(8,128)(2,1)} %param.14) | copy-start | bytes 786436
  7.2 99.8 %all-gather.6.cloned.1.call-start = ((), (), s32[]{:S(2)}) async-start(), calls=%async_computation.3 | async-start | bytes 7077888 | tf_op jit(solution)/shard_map/all_gather | solution.py:85
  7.9 263.9 %all-gather.4.cloned.1.call-start = ((), (), s32[]{:S(2)}) async-start(), calls=%async_computation.2 | async-start | bytes 4718592 | tf_op jit(solution)/shard_map/all_gather | solution.py:14
  25.3 11.0 %copy-start.2 = (f32[1024,32]{0,1:T(8,128)S(1)}, f32[1024,32]{0,1:T(8,128)}, u32[]{:S(2)}) copy-start(f32[1024,32]{0,1:T(8,128)} %param.11) | copy-start | bytes 393220
  25.3 11.1 %copy-start.1 = (bf16[1024,128]{1,0:T(8,128)(2,1)S(1)}, bf16[1024,128]{1,0:T(8,128)(2,1)}, u32[]{:S(2)}) copy-start(bf16[1024,128]{1,0:T(8,128)(2,1)} %param.13) | copy-start | bytes 786436
  41.5 274.4 %reduce-scatter.2.cloned.1.call-start = ((), (), s32[]{:S(2)}) async-start(), calls=%async_computation.4 | async-start | bytes 3932160 | tf_op jit(solution)/shard_map/reduce_scatter | solution.py:99
  238.2 2.2 copy-start.4
  271.9 9.7 %copy-start.3 = (f32[32]{0:T(128)S(1)}, f32[32]{0:T(128)}, u32[]{:S(2)}) copy-start(f32[32]{0:T(128)} %param.15) | copy-start | bytes 388
Sparse Core Ops, SparseCore 0:
  10.2 96.8 all-gather.5
  109.1 121.4 all-gather.3
  240.5 38.6 reduce-scatter.1
